TPU v7x, 8 devices: a whole 2x2x1 slice. The times are simulated.
8 devices in a mesh: data: 2 (over z, y), tp: 4 (over x, core).
Axes of the slice: x: 2, y: 2, z: 1, core: 2. Of those that a mesh axis runs over, the one named last changes fastest.
Arguments:
- x_all: bfloat16 [256, 4096], P(('data', 'tp')), parts along dimension 0
- ln_gammas: float32 [2, 4096], replicated
- w_in: bfloat16 [2, 4096, 16384], P(None, None, 'tp')
- w_out: bfloat16 [2, 16384, 4096], P(None, 'tp')
Outputs:
- output: bfloat16 [256, 4096], P(('data', 'tp')), parts along dimension 0
There are 2 independent parts. A program takes and returns all parts, laid end to end along the dimension named above; an argument that names none is the same for every part.
All inputs are finite; a program needn't handle non-finite values.
Results may differ from a plain program's by a relative error of at most 0.0100171.
Values are sent between devices in bfloat16 or wider.
A program may use at most 1 GiB of HBM per device.

v0:
```python
import jax
import jax.numpy as jnp
from jax import lax
from jax.sharding import PartitionSpec as P, NamedSharding

LN_EPS = 1e-6


def layer_norm(x_rows, gamma_row):
    x_f32 = x_rows.astype(jnp.float32)
    mean_val = jnp.mean(x_f32, axis=-1, keepdims=True)
    centered = x_f32 - mean_val
    var_val = jnp.mean(centered * centered, axis=-1, keepdims=True)
    return (centered * lax.rsqrt(var_val + LN_EPS) * gamma_row).astype(jnp.bfloat16)


def solution(mesh):
    def local_stack(x_local, ln_gammas, w_in, w_out):
        residual = x_local
        for layer_idx in range(w_in.shape[0]):
            normed = layer_norm(residual, ln_gammas[layer_idx])
            gathered = lax.all_gather(normed, 'tp', axis=0, tiled=True)
            hidden = jax.nn.gelu(jnp.dot(gathered, w_in[layer_idx], preferred_element_type=jnp.float32), approximate=True).astype(jnp.bfloat16)
            partial_out = jnp.dot(hidden, w_out[layer_idx], preferred_element_type=jnp.float32)
            reduced = lax.psum_scatter(partial_out, 'tp', scatter_dimension=0, tiled=True)
            residual = (residual.astype(jnp.float32) + reduced).astype(jnp.bfloat16)
        return residual

    return jax.shard_map(
        local_stack,
        mesh=mesh,
        in_specs=(P(('data', 'tp'), None), P(None, None), P(None, None, 'tp'), P(None, 'tp', None)),
        out_specs=P(('data', 'tp'), None),
        check_vma=False,
    )
```

profile of v0, /device:TPU:0, one launch (start us, length us, event | category | flops | bytes accessed | tf_op | source)
XLA Modules:
  0.0 153.4 jit_solution(17247672627907403979)
XLA Ops:
  6.5 0.0 all-gather.3.cloned.1.call-start
  6.5 1.1 convert_reduce_fusion.1
  7.6 1.2 fusion.55
  8.8 0.9 fusion.69
  9.7 1.8 %fusion.57 = bf16[32,4096]{1,0:T(8,128)(2,1)} fusion(bf16[32,4096]{1,0:T(8,128)(2,1)} %param.4, f32[4096]{0:T(1024)S(1)} %bitcast.29, f32[32]{0:T(128)S(1)} %add_rsqrt_fusion.1, f32[32]{0:T(128)S(1)} %broadcast_multiply_fusion.1), kind=kLoop, calls=%fused_computation.53 | loop fusion | flops 655360 | bytes 540928 | tf_op jit(solution)/shard_map/convert_element_type | solution.py:14
  11.5 0.0 all-gather.3.cloned.1.call-update
  11.5 0.0 reduce-scatter.3.cloned.1.call-start
  11.6 16.7 %all-gather.3.cloned.1.call-done = bf16[128,4096]{1,0:T(8,128)(2,1)} async-done(((bf16[32,4096]{1,0:T(8,128)(2,1)}), bf16[128,4096]{1,0:T(8,128)(2,1)}) %all-gather.3.cloned.1.call-update) | async-done | bytes 1048592 | tf_op jit(solution)/shard_map/all_gather | solution.py:22
  28.3 24.6 %fusion.4 = f32[128,4096]{1,0:T(8,128)} fusion(bf16[2,4096,4096]{2,1,0:T(8,128)(2,1)} %param.7, bf16[128,4096]{1,0:T(8,128)(2,1)} %all-gather.3.cloned.1.call-done, bf16[2,4096,4096]{2,1,0:T(8,128)(2,1)} %param.6), kind=kOutput, calls=%fused_computation.4 | convolution fusion | flops 8594653184 | bytes 70254592 | tf_op jit(solution)/shard_map/dot_general | solution.py:24
  52.9 0.0 copy-start
  52.9 0.0 reduce-scatter.3.cloned.1.call-update
  52.9 0.0 all-gather.5.cloned.1.call-start
  52.9 25.6 %reduce-scatter.3.cloned.1.call-done = f32[32,4096]{1,0:T(8,128)} async-done(((f32[128,4096]{1,0:T(8,128)}), f32[32,4096]{1,0:T(8,128)}) %reduce-scatter.3.cloned.1.call-update) | async-done | bytes 524304 | tf_op jit(solution)/shard_map/reduce_scatter | solution.py:25
  78.6 0.0 copy-done
  78.6 1.2 convert_reduce_fusion
  79.8 0.3 fusion.52
  80.0 0.9 fusion.54
  80.9 0.0 all-gather.5.cloned.1.call-update
  80.9 0.0 reduce-scatter.5.cloned.1.call-start
  81.0 13.8 %all-gather.5.cloned.1.call-done = bf16[128,4096]{1,0:T(8,128)(2,1)} async-done(((bf16[32,4096]{1,0:T(8,128)(2,1)}), bf16[128,4096]{1,0:T(8,128)(2,1)}) %all-gather.5.cloned.1.call-update) | async-done | bytes 1048592 | tf_op jit(solution)/shard_map/all_gather | solution.py:22
  94.8 24.6 %fusion = f32[128,4096]{1,0:T(8,128)} fusion(bf16[2,4096,4096]{2,1,0:T(8,128)(2,1)} %param.7, bf16[128,4096]{1,0:T(8,128)(2,1)} %all-gather.5.cloned.1.call-done, bf16[2,4096,4096]{2,1,0:T(8,128)(2,1)} %param.6), kind=kOutput, calls=%fused_computation | convolution fusion | flops 8594653184 | bytes 70254592 | tf_op jit(solution)/shard_map/dot_general | solution.py:24
  119.4 0.0 reduce-scatter.5.cloned.1.call-update
  119.4 25.7 %reduce-scatter.5.cloned.1.call-done = f32[32,4096]{1,0:T(8,128)} async-done(((f32[128,4096]{1,0:T(8,128)}), f32[32,4096]{1,0:T(8,128)}) %reduce-scatter.5.cloned.1.call-update) | async-done | bytes 524304 | tf_op jit(solution)/shard_map/reduce_scatter | solution.py:25
  145.1 1.8 %fusion.59 = bf16[32,4096]{1,0:T(8,128)(2,1)} fusion(f32[32,4096]{1,0:T(8,128)} %reduce-scatter.5.cloned.1.call-done, bf16[32,4096]{1,0:T(8,128)(2,1)S(1)} %get-tuple-element.6), kind=kLoop, calls=%fused_computation.55 | loop fusion | flops 393216 | bytes 1048576 | tf_op jit(solution)/shard_map/convert_element_type | solution.py:26
  (4 shorter events, 0.0 us)
Async XLA Ops:
  6.5 21.7 %all-gather.3.cloned.1.call-start = ((), (), s32[]{:S(2)}) async-start(), calls=%async_computation.2 | async-start | bytes 1310720 | tf_op jit(solution)/shard_map/all_gather | solution.py:22
  11.5 67.0 %reduce-scatter.3.cloned.1.call-start = ((), (), s32[]{:S(2)}) async-start(), calls=%async_computation.3 | async-start | bytes 2621440 | tf_op jit(solution)/shard_map/reduce_scatter | solution.py:25
  52.9 25.7 %copy-start = (bf16[32,4096]{1,0:T(8,128)(2,1)S(1)}, bf16[32,4096]{1,0:T(8,128)(2,1)}, u32[]{:S(2)}) copy-start(bf16[32,4096]{1,0:T(8,128)(2,1)} %param.4) | copy-start | bytes 786436
  52.9 41.9 %all-gather.5.cloned.1.call-start = ((), (), s32[]{:S(2)}) async-start(), calls=%async_computation.4 | async-start | bytes 1310720 | tf_op jit(solution)/shard_map/all_gather | solution.py:22
  80.9 64.2 %reduce-scatter.5.cloned.1.call-start = ((), (), s32[]{:S(2)}) async-start(), calls=%async_computation.5 | async-start | bytes 2621440 | tf_op jit(solution)/shard_map/reduce_scatter | solution.py:25
Sparse Core Ops, SparseCore 0:
  11.7 16.5 all-gather.2
  53.0 25.5 reduce-scatter.2
  81.1 13.7 all-gather.4
  119.5 25.5 reduce-scatter.4
where the time goes:
time: 154 us; the launch traced here: 153 us
  waiting for transfers between devices  81.9 us (53%)
  matrix products  49.2 us (32%)
  between operations  13.1 us (9%)
  other arithmetic  8.23 us (5%)
    reduce_scatter x2, waiting for transfers between devices, local_stack(): lax.psum_scatter(partial_out, 'tp', scatter_dimension=0, tiled=True)  51.3 us
    dot_general x2, matrix products, local_stack(): jnp.dot(hidden, w_out[layer_idx], preferred_element_type=jnp.float32)  49.2 us
    all_gather x2, waiting for transfers between devices, local_stack(): gathered = lax.all_gather(normed, 'tp', axis=0, tiled=True)  30.5 us
  transfers between devices with their start and end apart: 4, of which 4 were waited for; matrix products, arithmetic and copies ran while one was open for 0% of the time, Pallas kernels for 0%

commit v1 on v0

v1 whole, which is shorter than its diff:
```python
import functools

import jax
import jax.numpy as jnp
from jax import lax
from jax.experimental import pallas as pl
from jax.experimental.pallas import tpu as pltpu
from jax.sharding import PartitionSpec as P

LN_EPS = 1e-6
CHUNK = 512
W2_SLOTS = 5
MESH = pl.DeviceIdType.MESH
F32 = jnp.float32
BF16 = jnp.bfloat16


def gelu_tanh(u):
    c = 0.7978845608028654
    return 0.5 * u * (1.0 + jnp.tanh(c * (u + 0.044715 * (u * u * u))))


def mlp_kernel(
    x_hbm, g_hbm, w1_hbm, w2_hbm, out_hbm,
    res, gv, w1s, w2s, xn, u, h, pb, rb, sb, xr,
    in_sem, w1_sem, w2_sem, out_sem,
    agp_s, agp_r, agx_s, agx_r, agr_s, agr_r, dd_s, dd_r, lk_s, lk_r,
):
    layers, d_model, ff = w1_hbm.shape
    rows = x_hbm.shape[0]
    nc = d_model // CHUNK
    data_i = lax.axis_index("data")
    me = lax.axis_index("tp")
    core = lax.rem(me, 2)
    chip = lax.div(me, 2)
    partner = me + 1 - 2 * core
    xpeer = me + 2 - 4 * chip

    def w1_copy(l, k):
        return pltpu.make_async_copy(
            w1_hbm.at[l, pl.ds(pl.multiple_of(k * CHUNK, CHUNK), CHUNK), :], w1s.at[k], w1_sem.at[k])

    def w2_copy(l, n):
        slot = lax.rem(n + l * nc, W2_SLOTS)
        return pltpu.make_async_copy(
            w2_hbm.at[l, :, pl.ds(pl.multiple_of(n * CHUNK, CHUNK), CHUNK)], w2s.at[slot], w2_sem.at[slot])

    def remote(src, dst, ssem, rsem, to):
        return pltpu.make_async_remote_copy(
            src_ref=src, dst_ref=dst, send_sem=ssem, recv_sem=rsem,
            device_id=(data_i, to), device_id_type=MESH)

    def ag_partner(l, k):
        return remote(xn.at[k, me], xn.at[k, me], agp_s.at[l, k], agp_r.at[l, k], partner)

    def ag_x(l, k):
        return remote(xn.at[k, me], xn.at[k, me], agx_s.at[l, k], agx_r.at[l, k], xpeer)

    def ag_relay(l, k):
        return remote(xn.at[k, xpeer], xn.at[k, xpeer], agr_s.at[l, k], agr_r.at[l, k], partner)

    def rs_partner(l, n):
        return remote(pb.at[n, 1 - core], rb.at[n], dd_s.at[l, n], dd_r.at[l, n], partner)

    def rs_x(l, n):
        return remote(sb.at[n, 1 - chip], xr.at[n], lk_s.at[l, n], lk_r.at[l, n], xpeer)

    x_in = pltpu.make_async_copy(x_hbm, res, in_sem.at[0])
    g_in = pltpu.make_async_copy(g_hbm, gv, in_sem.at[1])
    x_in.start()
    g_in.start()
    for k in range(nc):
        w1_copy(0, k).start()
    for n in range(W2_SLOTS):
        w2_copy(0, n).start()

    barrier = pltpu.get_barrier_semaphore()
    for peer in (partner, xpeer):
        pl.semaphore_signal(barrier, inc=1, device_id=(data_i, peer), device_id_type=MESH)
    x_in.wait()
    g_in.wait()
    pl.semaphore_wait(barrier, 2)

    def cols(n):
        return pl.ds(n * CHUNK, CHUNK)

    for l in range(layers):
        total = res[:, cols(0)].astype(F32)
        for n in range(1, nc):
            total += res[:, cols(n)].astype(F32)
        mean = jnp.sum(total, axis=-1, keepdims=True) * (1.0 / d_model)
        total = None
        for n in range(nc):
            cen = res[:, cols(n)].astype(F32) - mean
            total = cen * cen if total is None else total + cen * cen
        var = jnp.sum(total, axis=-1, keepdims=True) * (1.0 / d_model)
        inv = lax.rsqrt(var + LN_EPS)
        for k in range(nc):
            cen = res[:, cols(k)].astype(F32) - mean
            xn[k, me] = (cen * inv * gv[pl.ds(l, 1), cols(k)]).astype(BF16)
            ag_x(l, k).start()
            ag_partner(l, k).start()

        def arrive(k):
            ag_x(l, k).wait_recv()
            ag_relay(l, k).start()

        def ready(k):
            ag_partner(l, k).wait_recv()
            ag_relay(l, k).wait_recv()
            w1_copy(l, k).wait()

        def w1_block(k, n):
            lhs = xn[k].reshape(4 * rows, CHUNK)
            return jnp.dot(lhs, w1s[k, :, cols(n)], preferred_element_type=F32)

        arrive(0)
        arrive(1)
        ready(0)
        for n in range(ff // CHUNK):
            u[:, cols(n)] = w1_block(0, n)

        @pl.loop(1, nc - 1)
        def _(k):
            arrive(k + 1)
            ready(k)
            for n in range(ff // CHUNK):
                u[:, cols(n)] += w1_block(k, n)

        ready(nc - 1)
        for n in range(ff // CHUNK):
            h[:, cols(n)] = gelu_tanh(u[:, cols(n)] + w1_block(nc - 1, n)).astype(BF16)

        for k in range(nc):
            ag_x(l, k).wait_send()
            ag_partner(l, k).wait_send()
            ag_relay(l, k).wait_send()

        def finish(n):
            rs_partner(l, n).wait()
            sb[n] = pb[n, core] + rb[n]
            rs_x(l, n).start()

        @pl.loop(0, nc)
        def _(n):
            w2_copy(l, n).wait()
            slot = lax.rem(n + l * nc, W2_SLOTS)
            acc = jnp.dot(h[...], w2s[slot], preferred_element_type=F32)
            for d in range(4):
                pb[n, d % 2, d // 2] = acc[d * rows:(d + 1) * rows]
            rs_partner(l, n).start()

            @pl.when(n + W2_SLOTS < nc)
            def _():
                w2_copy(l, n + W2_SLOTS).start()

            if l + 1 < layers:
                @pl.when(n + W2_SLOTS >= nc)
                def _():
                    w1_copy(l + 1, n + W2_SLOTS - nc).start()

            @pl.when(n > 0)
            def _():
                finish(n - 1)

        if l + 1 < layers:
            for k in range(W2_SLOTS, nc):
                w1_copy(l + 1, k).start()
            for n in range(W2_SLOTS):
                w2_copy(l + 1, n).start()
        finish(nc - 1)

        outs = []
        for n in range(nc):
            rs_x(l, n).wait()
            y = res[:, cols(n)].astype(F32) + (sb[n, chip] + xr[n])
            res[:, cols(n)] = y.astype(BF16)
            if l + 1 == layers:
                out = pltpu.make_async_copy(res.at[:, cols(n)], out_hbm.at[:, cols(n)], out_sem.at[n])
                out.start()
                outs.append(out)
        for out in outs:
            out.wait()


def solution(mesh):
    def local_stack(x_local, ln_gammas, w_in, w_out):
        rows, d_model = x_local.shape
        layers, _, ff = w_in.shape
        nc = d_model // CHUNK
        dma = pltpu.SemaphoreType.DMA
        pair = [dma((layers, nc)), dma((layers, nc))]
        return pl.pallas_call(
            mlp_kernel,
            out_shape=jax.ShapeDtypeStruct((rows, d_model), BF16),
            in_specs=[pl.BlockSpec(memory_space=pl.ANY)] * 4,
            out_specs=pl.BlockSpec(memory_space=pl.ANY),
            scratch_shapes=[
                pltpu.VMEM((rows, d_model), BF16),
                pltpu.VMEM(ln_gammas.shape, F32),
                pltpu.VMEM((nc, CHUNK, ff), BF16),
                pltpu.VMEM((W2_SLOTS, ff, CHUNK), BF16),
                pltpu.VMEM((nc, 4, rows, CHUNK), BF16),
                pltpu.VMEM((4 * rows, ff), F32),
                pltpu.VMEM((4 * rows, ff), BF16),
                pltpu.VMEM((nc, 2, 2, rows, CHUNK), F32),
                pltpu.VMEM((nc, 2, rows, CHUNK), F32),
                pltpu.VMEM((nc, 2, rows, CHUNK), F32),
                pltpu.VMEM((nc, rows, CHUNK), F32),
                dma((2,)), dma((nc,)), dma((W2_SLOTS,)), dma((nc,)),
            ] + pair * 5,
            compiler_params=pltpu.CompilerParams(
                collective_id=0, has_side_effects=True, vmem_limit_bytes=67043328),
            name="mlp_stack",
        )(x_local, ln_gammas, w_in, w_out)

    return jax.shard_map(
        local_stack,
        mesh=mesh,
        in_specs=(P(('data', 'tp'), None), P(None, None), P(None, None, 'tp'), P(None, 'tp', None)),
        out_specs=P(('data', 'tp'), None),
        check_vma=False,
    )
```

time: 154 us -> 72.3 us (0.47)
  waiting for transfers between devices: 81.9 us -> 0 us
  Pallas kernels: 0 us -> 70.5 us
  matrix products: 49.2 us -> 0 us
  between operations: 13.1 us -> 0.01 us
  other arithmetic: 8.23 us -> 0 us
    pallas_call x0 -> x1, Pallas kernels: none -> 70.5 us  [local_stack(): pl.pallas_call(mlp_kernel, out_shape=jax.ShapeDtypeStruct((rows, d_model)...]
    reduce_scatter x2 -> x0, waiting for transfers between devices: 51.3 us -> none  [local_stack(): lax.psum_scatter(partial_out, 'tp', scatter_dimension=0, tiled=True)]
    dot_general x2 -> x0, matrix products: 49.2 us -> none  [local_stack(): jnp.dot(hidden, w_out[layer_idx], preferred_element_type=jnp.float32)]
    all_gather x2 -> x0, waiting for transfers between devices: 30.5 us -> none  [local_stack(): gathered = lax.all_gather(normed, 'tp', axis=0, tiled=True)]
    convert_element_type x3 -> x0, other arithmetic: 4.45 us -> none  [the longest x2 2.66 us: layer_norm(): (centered * lax.rsqrt(var_val + LN_EPS) * gamma_row).astype(jnp.bfloat16)]
    reduce_sum x4 -> x0, other arithmetic: 3.76 us -> none  [the longest x2 2.3 us: layer_norm(): mean_val = jnp.mean(x_f32, axis=-1, keepdims=True)]
    unnamed x2 -> x1, local copies, waits for them, and re-layouts: 0.01 us -> 1.67 us
  transfers between devices with their start and end apart: 4 -> 0, of which waited for: 4 -> 0; matrix products, arithmetic and copies ran while one was open for 0% -> 0% of each run, Pallas kernels for 0% -> 0%
where the time goes in v1:
time: 72.3 us; the launch traced here: 72.2 us
  Pallas kernels  70.5 us (98%)
  local copies, waits for them, and re-layouts  1.67 us (2%)
    pallas_call x1, Pallas kernels, local_stack(): pl.pallas_call(mlp_kernel, out_shape=jax.ShapeDtypeStruct((rows, d_model)...  70.5 us
    unnamed x1, local copies, waits for them, and re-layouts  1.67 us

profile of v1, /device:TPU:0, one launch (start us, length us, event | category | flops | bytes accessed | tf_op | source)
XLA Modules:
  0.0 72.2 jit_solution(945463704991641109)
XLA Ops:
  0.0 70.5 %mlp_stack.1 = bf16[32,4096]{1,0:T(8,128)(2,1)} custom-call(bf16[32,4096]{1,0:T(8,128)(2,1)} %x_hbm.1, f32[2,4096]{1,0:T(2,128)} %g_hbm.1, bf16[2,4096,4096]{2,1,0:T(8,128)(2,1)} %w1_hbm.1, bf16[2,4096,4096]{2,1,0:T(8,128)(2,1)} %w2_hbm.1), custom_call_target="tpu_custom_call" | custom-call | tf_op jit(solution)/shard_map/mlp_stack/pallas_call | solution.py:193
  70.6 1.7 %copy.6 = bf16[32,4096]{1,0:T(8,128)(2,1)} copy(bf16[32,4096]{1,0:T(8,128)(2,1)} %mlp_stack.1) | data formatting | bytes 524288

commit v2 on v1

v2 whole, which is shorter than its diff:
```python
import functools

import jax
import jax.numpy as jnp
from jax import lax
from jax.experimental import pallas as pl
from jax.experimental.pallas import tpu as pltpu
from jax.sharding import PartitionSpec as P

LN_EPS = 1e-6
CHUNK = 512
PART = 256
W2_SLOTS = 5
MESH = pl.DeviceIdType.MESH
F32 = jnp.float32
BF16 = jnp.bfloat16


def gelu_tanh(u):
    c = 0.7978845608028654
    return 0.5 * u * (1.0 + jnp.tanh(c * (u + 0.044715 * (u * u * u))))


def mlp_kernel(
    x_hbm, g_hbm, w1_hbm, w2_hbm, out_ref,
    res, gv, w1s, w2s, xn, u, h, pb, rb, sb, xr,
    in_sem, w1_sem, w2_sem,
    agp_s, agp_r, agx_s, agx_r, agr_s, agr_r, dd_s, dd_r, lk_s, lk_r,
):
    layers, d_model, ff = w1_hbm.shape
    rows = x_hbm.shape[0]
    nc = d_model // CHUNK
    halves = CHUNK // PART
    data_i = lax.axis_index("data")
    me = lax.axis_index("tp")
    core = lax.rem(me, 2)
    chip = lax.div(me, 2)
    partner = me + 1 - 2 * core
    xpeer = me + 2 - 4 * chip

    def w1_copy(l, k):
        return pltpu.make_async_copy(
            w1_hbm.at[l, pl.ds(pl.multiple_of(k * CHUNK, CHUNK), CHUNK), :], w1s.at[k], w1_sem.at[k])

    def w2_copy(l, n):
        slot = lax.rem(n + l * nc, W2_SLOTS)
        return pltpu.make_async_copy(
            w2_hbm.at[l, :, pl.ds(pl.multiple_of(n * CHUNK, CHUNK), CHUNK)], w2s.at[slot], w2_sem.at[slot])

    def remote(src, dst, ssem, rsem, to):
        return pltpu.make_async_remote_copy(
            src_ref=src, dst_ref=dst, send_sem=ssem, recv_sem=rsem,
            device_id=(data_i, to), device_id_type=MESH)

    def ag_partner(k):
        return remote(xn.at[k, me], xn.at[k, me], agp_s.at[0], agp_r.at[k], partner)

    def ag_x(k):
        return remote(xn.at[k, me], xn.at[k, me], agx_s.at[0], agx_r.at[k], xpeer)

    def ag_relay(k):
        return remote(xn.at[k, xpeer], xn.at[k, xpeer], agr_s.at[0], agr_r.at[k], partner)

    def rs_partner(j):
        return remote(pb.at[j, 1 - core], rb.at[j], dd_s.at[0], dd_r.at[j], partner)

    def rs_x(j):
        return remote(sb.at[j, 1 - chip], xr.at[j], lk_s.at[0], lk_r.at[j], xpeer)

    x_in = pltpu.make_async_copy(x_hbm, res, in_sem.at[0])
    g_in = pltpu.make_async_copy(g_hbm, gv, in_sem.at[1])
    x_in.start()
    g_in.start()
    w1_copy(0, nc - 1).start(priority=1)
    barrier = pltpu.get_barrier_semaphore()
    for peer in (partner, xpeer):
        pl.semaphore_signal(barrier, inc=1, device_id=(data_i, peer), device_id_type=MESH)
    x_in.wait()
    g_in.wait()
    for k in range(nc - 1):
        w1_copy(0, k).start()
    for n in range(W2_SLOTS):
        w2_copy(0, n).start(priority=1)

    def cols(n, width=CHUNK):
        return pl.ds(n * width, width)

    total = None
    for n in range(nc):
        y = res[:, cols(n)].astype(F32)
        total = y if total is None else total + y

    for l in range(layers):
        mean = jnp.sum(total, axis=-1, keepdims=True) * (1.0 / d_model)
        total = None
        for n in range(nc):
            cen = res[:, cols(n)].astype(F32) - mean
            total = cen * cen if total is None else total + cen * cen
        var = jnp.sum(total, axis=-1, keepdims=True) * (1.0 / d_model)
        inv = lax.rsqrt(var + LN_EPS)
        if l == 0:
            pl.semaphore_wait(barrier, 2)
        for k in range(nc):
            cen = res[:, cols(k)].astype(F32) - mean
            xn[k, me] = (cen * inv * gv[pl.ds(l, 1), cols(k)]).astype(BF16)
            ag_x(k).start()
            ag_partner(k).start()

        def arrive(k):
            ag_x(k).wait_recv()
            ag_relay(k).start()

        def ready(k):
            ag_partner(k).wait_recv()
            ag_relay(k).wait_recv()
            w1_copy(l, k).wait()

        def w1_block(k, n):
            lhs = xn[k].reshape(4 * rows, CHUNK)
            return jnp.dot(lhs, w1s[k, :, cols(n)], preferred_element_type=F32)

        arrive(0)
        arrive(1)
        ready(0)
        for n in range(ff // CHUNK):
            u[:, cols(n)] = w1_block(0, n)

        @pl.loop(1, nc - 1)
        def _(k):
            arrive(k + 1)
            ready(k)
            for n in range(ff // CHUNK):
                u[:, cols(n)] += w1_block(k, n)

        ready(nc - 1)
        for n in range(ff // CHUNK):
            h[:, cols(n)] = gelu_tanh(u[:, cols(n)] + w1_block(nc - 1, n)).astype(BF16)

        remote(xn.at[:, me], xn.at[:, me], agx_s.at[0], agx_r.at[0], xpeer).wait_send()
        remote(xn.at[:, me], xn.at[:, me], agp_s.at[0], agp_r.at[0], partner).wait_send()
        remote(xn.at[:, me], xn.at[:, me], agr_s.at[0], agr_r.at[0], partner).wait_send()

        def finish(j):
            rs_partner(j).wait_recv()
            sb[j] = pb[j, core] + rb[j]
            rs_x(j).start()

        @pl.loop(0, nc)
        def _(n):
            w2_copy(l, n).wait()
            slot = lax.rem(n + l * nc, W2_SLOTS)
            acc = jnp.dot(h[...], w2s[slot], preferred_element_type=F32)
            for s in range(halves):
                for d in range(4):
                    pb[n * halves + s, d % 2, d // 2] = acc[d * rows:(d + 1) * rows, s * PART:(s + 1) * PART]
                rs_partner(n * halves + s).start()

            @pl.when(n > 0)
            def _():
                for s in range(halves):
                    finish((n - 1) * halves + s)

            @pl.when(n + W2_SLOTS < nc)
            def _():
                w2_copy(l, n + W2_SLOTS).start(priority=1)

            if l + 1 < layers:
                @pl.when(n + W2_SLOTS >= nc)
                def _():
                    w1_copy(l + 1, n + W2_SLOTS - nc).start(priority=1)

        if l + 1 < layers:
            for k in range(W2_SLOTS, nc):
                w1_copy(l + 1, k).start()
            for n in range(W2_SLOTS):
                w2_copy(l + 1, n).start(priority=1)
        for s in range(halves):
            finish((nc - 1) * halves + s)

        remote(pb.at[:, 0], rb, dd_s.at[0], dd_r.at[0], partner).wait_send()

        total = None
        for j in range(nc * halves):
            rs_x(j).wait_recv()
            y = res[:, cols(j, PART)].astype(F32) + (sb[j, chip] + xr[j])
            y = y.astype(BF16)
            res[:, cols(j, PART)] = y
            y = y.astype(F32)
            total = y if total is None else total + y
        remote(sb.at[:, 0], xr, lk_s.at[0], lk_r.at[0], xpeer).wait_send()
    out_ref[...] = res[...]


def solution(mesh):
    def local_stack(x_local, ln_gammas, w_in, w_out):
        rows, d_model = x_local.shape
        layers, _, ff = w_in.shape
        nc = d_model // CHUNK
        dma = pltpu.SemaphoreType.DMA
        parts = d_model // PART
        return pl.pallas_call(
            mlp_kernel,
            out_shape=pltpu.VMEM((rows, d_model), BF16),
            in_specs=[pl.BlockSpec(memory_space=pl.ANY)] * 4,
            out_specs=pl.BlockSpec(memory_space=pltpu.VMEM),
            scratch_shapes=[
                pltpu.VMEM((rows, d_model), BF16),
                pltpu.VMEM(ln_gammas.shape, F32),
                pltpu.VMEM((nc, CHUNK, ff), BF16),
                pltpu.VMEM((W2_SLOTS, ff, CHUNK), BF16),
                pltpu.VMEM((nc, 4, rows, CHUNK), BF16),
                pltpu.VMEM((4 * rows, ff), F32),
                pltpu.VMEM((4 * rows, ff), BF16),
                pltpu.VMEM((parts, 2, 2, rows, PART), F32),
                pltpu.VMEM((parts, 2, rows, PART), F32),
                pltpu.VMEM((parts, 2, rows, PART), F32),
                pltpu.VMEM((parts, rows, PART), F32),
                dma((2,)), dma((nc,)), dma((W2_SLOTS,)),
                dma((1,)), dma((nc,)), dma((1,)), dma((nc,)), dma((1,)), dma((nc,)),
                dma((1,)), dma((parts,)), dma((1,)), dma((parts,)),
            ],
            compiler_params=pltpu.CompilerParams(
                collective_id=0, has_side_effects=True, vmem_limit_bytes=65536000),
            name="mlp_stack",
        )(x_local, ln_gammas, w_in, w_out)

    return jax.shard_map(
        local_stack,
        mesh=mesh,
        in_specs=(P(('data', 'tp'), None), P(None, None), P(None, None, 'tp'), P(None, 'tp', None)),
        out_specs=P(('data', 'tp'), None),
        check_vma=False,
    )
```

time: 72.3 us -> 58.2 us (0.80)
  Pallas kernels: 70.5 us -> 57.4 us
  local copies, waits for them, and re-layouts: 1.67 us -> 0.71 us
    pallas_call x1, Pallas kernels: 70.5 us -> 57.4 us  [local_stack(): pl.pallas_call(mlp_kernel, out_shape=pltpu.VMEM((rows, d_model), BF16), i...]
    unnamed x1, local copies, waits for them, and re-layouts: 1.67 us -> 0.71 us
where the time goes in v2:
time: 58.2 us; the launch traced here: 58.1 us
  Pallas kernels  57.4 us (99%)
  local copies, waits for them, and re-layouts  0.71 us (1%)
    pallas_call x1, Pallas kernels, local_stack(): pl.pallas_call(mlp_kernel, out_shape=pltpu.VMEM((rows, d_model), BF16), i...  57.4 us

profile of v2, /device:TPU:0, one launch (start us, length us, event | category | flops | bytes accessed | tf_op | source)
XLA Modules:
  0.0 58.1 jit_solution(1013038340586165799)
XLA Ops:
  0.0 57.4 %mlp_stack.1 = bf16[32,4096]{1,0:T(8,128)(2,1)S(1)} custom-call(bf16[32,4096]{1,0:T(8,128)(2,1)} %x_hbm.1, f32[2,4096]{1,0:T(2,128)} %g_hbm.1, bf16[2,4096,4096]{2,1,0:T(8,128)(2,1)} %w1_hbm.1, bf16[2,4096,4096]{2,1,0:T(8,128)(2,1)} %w2_hbm.1), custom_call_target="tpu_custom_call" | custom-call | tf_op jit(solution)/shard_map/mlp_stack/pallas_call | solution.py:201
  57.4 0.7 %copy.6 = bf16[32,4096]{1,0:T(8,128)(2,1)} copy(bf16[32,4096]{1,0:T(8,128)(2,1)S(1)} %mlp_stack.1) | data formatting | bytes 524288

commit v3 on v2

--- a/solution.py
+++ b/solution.py
@@ -18,7 +18,7 @@
 
 def gelu_tanh(u):
     c = 0.7978845608028654
-    return 0.5 * u * (1.0 + jnp.tanh(c * (u + 0.044715 * (u * u * u))))
+    return (0.5 * u) * (1.0 + jnp.tanh(u * (c + (c * 0.044715) * (u * u))))
 
 
 def mlp_kernel(
@@ -38,6 +38,9 @@
     partner = me + 1 - 2 * core
     xpeer = me + 2 - 4 * chip
 
+    def cols(n, width=CHUNK):
+        return pl.ds(n * width, width)
+
     def w1_copy(l, k):
         return pltpu.make_async_copy(
             w1_hbm.at[l, pl.ds(pl.multiple_of(k * CHUNK, CHUNK), CHUNK), :], w1s.at[k], w1_sem.at[k])
@@ -71,19 +74,16 @@
     g_in = pltpu.make_async_copy(g_hbm, gv, in_sem.at[1])
     x_in.start()
     g_in.start()
-    w1_copy(0, nc - 1).start(priority=1)
+    w1_copy(0, 0).start(priority=1)
     barrier = pltpu.get_barrier_semaphore()
     for peer in (partner, xpeer):
         pl.semaphore_signal(barrier, inc=1, device_id=(data_i, peer), device_id_type=MESH)
     x_in.wait()
     g_in.wait()
-    for k in range(nc - 1):
+    for k in range(1, nc):
         w1_copy(0, k).start()
     for n in range(W2_SLOTS):
         w2_copy(0, n).start(priority=1)
-
-    def cols(n, width=CHUNK):
-        return pl.ds(n * width, width)
 
     total = None
     for n in range(nc):
@@ -132,34 +132,24 @@
             for n in range(ff // CHUNK):
                 u[:, cols(n)] += w1_block(k, n)
 
-        ready(nc - 1)
-        for n in range(ff // CHUNK):
-            h[:, cols(n)] = gelu_tanh(u[:, cols(n)] + w1_block(nc - 1, n)).astype(BF16)
-
-        remote(xn.at[:, me], xn.at[:, me], agx_s.at[0], agx_r.at[0], xpeer).wait_send()
-        remote(xn.at[:, me], xn.at[:, me], agp_s.at[0], agp_r.at[0], partner).wait_send()
-        remote(xn.at[:, me], xn.at[:, me], agr_s.at[0], agr_r.at[0], partner).wait_send()
-
         def finish(j):
             rs_partner(j).wait_recv()
             sb[j] = pb[j, core] + rb[j]
             rs_x(j).start()
 
-        @pl.loop(0, nc)
-        def _(n):
-            w2_copy(l, n).wait()
-            slot = lax.rem(n + l * nc, W2_SLOTS)
-            acc = jnp.dot(h[...], w2s[slot], preferred_element_type=F32)
+        def partial_sums(n, slot):
+            send_partial(n, jnp.dot(h[...], w2s[slot], preferred_element_type=F32))
+
+        def send_partial(n, acc):
             for s in range(halves):
-                for d in range(4):
-                    pb[n * halves + s, d % 2, d // 2] = acc[d * rows:(d + 1) * rows, s * PART:(s + 1) * PART]
-                rs_partner(n * halves + s).start()
-
-            @pl.when(n > 0)
-            def _():
-                for s in range(halves):
-                    finish((n - 1) * halves + s)
-
+                send_part(n * halves + s, acc[:, s * PART:(s + 1) * PART])
+
+        def send_part(j, acc):
+            for d in range(4):
+                pb[j, d % 2, d // 2] = acc[d * rows:(d + 1) * rows]
+            rs_partner(j).start()
+
+        def refill(n):
             @pl.when(n + W2_SLOTS < nc)
             def _():
                 w2_copy(l, n + W2_SLOTS).start(priority=1)
@@ -168,6 +158,41 @@
                 @pl.when(n + W2_SLOTS >= nc)
                 def _():
                     w1_copy(l + 1, n + W2_SLOTS - nc).start(priority=1)
+
+        slot = (l * nc) % W2_SLOTS
+        ready(nc - 1)
+        if l == 0:
+            for n in range(ff // CHUNK):
+                h[:, cols(n)] = gelu_tanh(u[:, cols(n)] + w1_block(nc - 1, n)).astype(BF16)
+            w2_copy(l, 0).wait()
+            acc = jnp.dot(h[...], w2s[slot], preferred_element_type=F32)
+        else:
+            w2_copy(l, 0).wait()
+            acc, ahead = None, None
+            for n in range(ff // CHUNK + 1):
+                here = None
+                if n < ff // CHUNK:
+                    here = gelu_tanh(u[:, cols(n)] + w1_block(nc - 1, n)).astype(BF16)
+                    h[:, cols(n)] = here
+                if n > 0:
+                    part = jnp.dot(ahead, w2s[slot, cols(n - 1), :], preferred_element_type=F32)
+                    acc = part if acc is None else acc + part
+                ahead = here
+        send_partial(0, acc)
+        refill(0)
+
+        remote(xn.at[:, me], xn.at[:, me], agx_s.at[0], agx_r.at[0], xpeer).wait_send()
+        remote(xn.at[:, me], xn.at[:, me], agp_s.at[0], agp_r.at[0], partner).wait_send()
+        remote(xn.at[:, me], xn.at[:, me], agr_s.at[0], agr_r.at[0], partner).wait_send()
+
+        @pl.loop(1, nc)
+        def _(n):
+            w2_copy(l, n).wait()
+            partial_sums(n, lax.rem(n + l * nc, W2_SLOTS))
+            refill(n)
+
+            for s in range(halves):
+                finish((n - 1) * halves + s)
 
         if l + 1 < layers:
             for k in range(W2_SLOTS, nc):

time: 58.2 us -> 57.2 us (0.983)
  Pallas kernels: 57.4 us -> 56.4 us
    pallas_call x1, Pallas kernels: 57.4 us -> 56.4 us  [local_stack(): pl.pallas_call(mlp_kernel, out_shape=pltpu.VMEM((rows, d_model), BF16), i...]
where the time goes in v3:
time: 57.2 us; the launch traced here: 57.1 us
  Pallas kernels  56.4 us (99%)
  local copies, waits for them, and re-layouts  0.71 us (1%)
    pallas_call x1, Pallas kernels, local_stack(): pl.pallas_call(mlp_kernel, out_shape=pltpu.VMEM((rows, d_model), BF16), i...  56.4 us

profile of v3, /device:TPU:0, one launch (start us, length us, event | category | flops | bytes accessed | tf_op | source)
XLA Modules:
  0.0 57.1 jit_solution(6452208661929280455)
XLA Ops:
  0.0 56.4 %mlp_stack.1 = bf16[32,4096]{1,0:T(8,128)(2,1)S(1)} custom-call(bf16[32,4096]{1,0:T(8,128)(2,1)} %x_hbm.1, f32[2,4096]{1,0:T(2,128)} %g_hbm.1, bf16[2,4096,4096]{2,1,0:T(8,128)(2,1)} %w1_hbm.1, bf16[2,4096,4096]{2,1,0:T(8,128)(2,1)} %w2_hbm.1), custom_call_target="tpu_custom_call" | custom-call | tf_op jit(solution)/shard_map/mlp_stack/pallas_call | solution.py:226
  56.4 0.7 %copy.6 = bf16[32,4096]{1,0:T(8,128)(2,1)} copy(bf16[32,4096]{1,0:T(8,128)(2,1)S(1)} %mlp_stack.1) | data formatting | bytes 524288
